TPU v7x, 32 devices: a whole 2x2x4 slice. The times are simulated.
32 devices in a mesh: grp: 2 (over x), slab: 16 (over z, y, core).
Axes of the slice: x: 2, y: 2, z: 4, core: 2. Of those that a mesh axis runs over, the one named last changes fastest.
Arguments:
- volume: bfloat16 [64, 1024, 1024], P(('grp', 'slab')), parts along dimension 0, may hold values from -60 to 60
- plane_shift: int32 [4, 32], P('grp', 'slab'), parts along dimension 0, may hold values from -64 to 64
- plane_weight: float32 [4, 32], P('grp', 'slab'), parts along dimension 0, may hold values from 0 to 1
- column_left: int32 [4, 1024], P('grp'), parts along dimension 0, may hold values from 0 to 1022
- column_weight: float32 [4, 1024], P('grp'), parts along dimension 0, may hold values from 0 to 1
- window_center: int32 [4, 2], P('grp'), parts along dimension 0, may hold values from -200 to 199
- tilt_owner: int32 [32], P('grp'), parts along dimension 0, may hold values from 0 to 15, each once
- reference_band: float32 [32, 2, 128, 128], P(('grp', 'slab')), parts along dimension 0, may hold values from -6 to 6
Outputs:
- correlation: float32 [4, 16, 128], P('grp', 'slab'), parts along dimension 0
- peaks: float32 [4], P('grp'), parts along dimension 0
There are 2 independent parts, one for each index of `grp`. A program takes and returns all parts, laid end to end along the dimension named above; each array names one. Nothing has to cross between parts.
Inputs may be any that keep to these rules, and one draw needn't show every extreme that they name: `tilt_owner`: the first 2 entries name the owners of the tilts, one slab index each.
All inputs are finite; a program needn't handle non-finite values.
Results may differ from a plain program's by a relative error of at most 0.0003.
Values sent between devices are 32-bit elements; how exact they have to be, the bound alone decides.
A program may use at most 128 MiB of HBM per device.

v0:
```python
import math
import jax
import jax.numpy as jnp
from jax import lax
from jax.sharding import PartitionSpec as P

Y = 1024
X = 1024
BAND = 128
WIN_COLS = 128
TILTS = 2
WIN_ROWS_DEV = 1


def from_root(value, axis, source):
    kept = jnp.where(lax.axis_index(axis) == source, value, 0).astype(value.dtype)
    return lax.psum(kept, axis)


def phase_pair(left_ints, right_ints, length):
    product = left_ints[:, None] * right_ints[None, :] % length
    angle = product.astype(jnp.float32) * (2.0 * math.pi / length)
    return (jnp.cos(angle), jnp.sin(angle))


def matmul(first, second):
    return jnp.dot(
        first, second, precision=lax.Precision.HIGHEST, preferred_element_type=jnp.float32
    )


def reproject(volume, shifts, weights, left_cols, right_share, row_count):
    grid_width = volume.shape[2]
    margin = grid_width // 16 + 1
    padded_all = jnp.pad(volume, ((0, 0), (0, 0), (margin, margin)))
    summed = jnp.zeros((row_count, grid_width), jnp.float32)
    for plane_no in range(volume.shape[0]):
        padded = padded_all[plane_no]
        near_cells = lax.dynamic_slice_in_dim(
            padded, margin - shifts[plane_no], grid_width, 1
        ).astype(jnp.float32)
        far_cells = lax.dynamic_slice_in_dim(
            padded, margin - shifts[plane_no] - 1, grid_width, 1
        ).astype(jnp.float32)
        summed = summed + (1.0 - weights[plane_no]) * near_cells + weights[plane_no] * far_cells
    left_values = jnp.take(summed, left_cols, axis=1)
    right_values = jnp.take(summed, left_cols + 1, axis=1)
    return (1.0 - right_share) * left_values + right_share * right_values


def band_part(projected):
    row_count, grid_width = projected.shape
    freq_cols = jnp.arange(BAND, dtype=jnp.int32)
    freq_rows = freq_cols - BAND // 2
    col_cos, col_sin = phase_pair(jnp.arange(grid_width, dtype=jnp.int32), freq_cols, grid_width)
    real_half = matmul(projected, col_cos)
    imag_half = -matmul(projected, col_sin)
    row_ids = jnp.arange(row_count, dtype=jnp.int32)
    row_cos, row_sin = phase_pair(freq_rows, row_ids, Y)
    spec_real = matmul(row_cos, real_half) + matmul(row_sin, imag_half)
    spec_imag = matmul(row_cos, imag_half) - matmul(row_sin, real_half)
    return jnp.stack([spec_real, spec_imag])


def correlate(spectrum, owned, center, row_ids, total_rows):
    spec_real, spec_imag = (spectrum[0], spectrum[1])
    ref_real, ref_imag = (owned[0], owned[1])
    cross_real = spec_real * ref_real + spec_imag * ref_imag
    cross_imag = spec_imag * ref_real - spec_real * ref_imag
    energy_spec = jnp.mean(spec_real * spec_real + spec_imag * spec_imag) + 1e-06
    energy_ref = jnp.mean(ref_real * ref_real + ref_imag * ref_imag) + 1e-06
    freq_cols = jnp.arange(BAND, dtype=jnp.int32)
    freq_rows = freq_cols - BAND // 2
    offsets_y = center[0] + row_ids - total_rows // 2
    offsets_x = center[1] + jnp.arange(WIN_COLS, dtype=jnp.int32) - WIN_COLS // 2
    row_cos, row_sin = phase_pair(offsets_y, freq_rows, Y)
    col_cos, col_sin = phase_pair(freq_cols, offsets_x, X)
    half_real = matmul(row_cos, cross_real) - matmul(row_sin, cross_imag)
    half_imag = matmul(row_cos, cross_imag) + matmul(row_sin, cross_real)
    return (matmul(half_real, col_cos) - matmul(half_imag, col_sin)) / (
        BAND * jnp.sqrt(energy_spec * energy_ref)
    )


def per_device(
    volume,
    plane_shift,
    plane_weight,
    column_left,
    column_weight,
    window_center,
    tilt_owner,
    reference_band,
):
    devices = lax.axis_size("slab")
    position = lax.axis_index("slab")
    partials = []
    for which in range(TILTS):

        def rows_term(first_row, row_count, which=which):
            return reproject(
                volume,
                plane_shift[which],
                plane_weight[which],
                column_left[which],
                column_weight[which],
                row_count,
            )

        partials.append(band_part(rows_term(0, Y)))
    stacked = jnp.stack(partials)
    mine = reference_band[0]
    spectra = lax.psum(stacked, "slab")
    references = jnp.stack([from_root(mine, "slab", tilt_owner[which]) for which in range(TILTS)])
    total_rows = WIN_ROWS_DEV * devices
    outputs = []
    maxima = []
    row_ids = position * WIN_ROWS_DEV + jnp.arange(WIN_ROWS_DEV, dtype=jnp.int32)
    for which in range(TILTS):
        corr = correlate(
            spectra[which], references[which], window_center[which], row_ids, total_rows
        )
        outputs.append(corr)
        maxima.append(jnp.max(corr))
    peaks = lax.pmax(jnp.stack(maxima), "slab")
    return (jnp.stack(outputs), peaks)


def solution(mesh):
    placed = (
        P(("grp", "slab"), None, None),
        P("grp", "slab"),
        P("grp", "slab"),
        P("grp", None),
        P("grp", None),
        P("grp", None),
        P("grp"),
        P(("grp", "slab"), None, None, None),
    )
    return jax.shard_map(
        per_device,
        mesh=mesh,
        in_specs=placed,
        out_specs=(P("grp", "slab", None), P("grp")),
        check_vma=False,
    )
```

profile of v0, /device:TPU:0, one launch (start us, length us, event | category | flops | bytes accessed | tf_op | source)
XLA Modules:
  0.0 311.6 jit_solution(11527147601551082680)
XLA Ops:
  24.0 6.2 %copy.10 = bf16[2,1024,1024]{1,2,0:T(8,128)(2,1)} copy(bf16[2,1024,1024]{2,1,0:T(8,128)(2,1)} %param.10) | data formatting | bytes 8388608 | tf_op args[0]
  30.2 5.0 %pad_slice_fusion.1 = (bf16[1,1024,1154]{1,2,0:T(8,128)(2,1)S(1)}, bf16[1,1024,1154]{1,2,0:T(8,128)(2,1)}) fusion(bf16[2,1024,1024]{1,2,0:T(8,128)(2,1)} %copy.10), kind=kLoop, calls=%fused_computation.5 | loop fusion | bytes 8921088 | tf_op jit(solution)/shard_map/slice | solution.py:38
  35.2 12.6 %add_bitcast_fusion.1 = (f32[1024,1024]{0,1:T(8,128)}, f32[1024,1024]{0,1:T(8,128)}) fusion(bf16[1,1024,1154]{1,2,0:T(8,128)(2,1)} %get-tuple-element.11, s32[]{:T(128)S(6)} %select_n.127, f32[]{:T(128)} %bitcast.11, s32[]{:T(128)S(6)} %select_n.126, f32[]{:T(128)S(6)} %sub.140, bf16[1,1024,1154]{1,2,0:T(8,128)(2,1)S(1)} %get-tuple-element.10, ...), kind=kLoop, calls=%fused_computation.13 | loop fusion | flops 23068672 | bytes 25165888 | tf_op jit(solution)/shard_map/add | solution.py:45
  47.8 8.6 %gather_fusion.2 = f32[1024,1024]{1,0:T(8,128)} fusion(f32[1024,1024]{0,1:T(8,128)} %get-tuple-element.9, s32[1024]{0:T(1024)S(1)} %get-tuple-element.34), kind=kCustom, calls=%fused_computation.2.clone | custom fusion | bytes 8392704 | tf_op jit(solution)/shard_map/jit(_take)/gather | solution.py:46
  56.4 8.6 %gather_fusion.3 = f32[1024,1024]{1,0:T(8,128)} fusion(f32[1024,1024]{0,1:T(8,128)} %get-tuple-element.9, s32[1024]{0:T(1024)S(1)} %get-tuple-element.35), kind=kCustom, calls=%fused_computation.3.clone | custom fusion | bytes 8392704 | tf_op jit(solution)/shard_map/jit(_take)/gather | solution.py:47
  65.0 4.4 %fusion = f32[1024,1024]{0,1:T(8,128)S(1)} fusion(f32[1024,1024]{1,0:T(8,128)} %gather_fusion.3, f32[1024,1024]{1,0:T(8,128)} %gather_fusion.2, f32[1024]{0:T(1024)S(1)} %bitcast.250, f32[1024]{0:T(1024)S(1)} %bitcast.249, pred[1024]{0:T(1024)(128)(4,1)S(1)} %get-tuple-element.33, pred[1024]{0:T(1024)(128)(4,1)S(1)} %get-tuple-element.32), kind=kLoop, calls=%fused_computation.7 | loop fusion | flops 5242880 | bytes 12593152 | tf_op jit(solution)/shard_map/add | solution.py:48
  69.4 8.5 %fusion.32 = f32[1024,128]{1,0:T(8,128)S(1)} fusion(f32[1024,1024]{0,1:T(8,128)S(1)} %fusion), kind=kOutput, calls=%fused_computation.69 | convolution fusion | flops 1612447744 | bytes 4718592 | tf_op jit(solution)/shard_map/dot_general | solution.py:27
  77.9 21.3 %convolution_negate_fusion = f32[1024,128]{1,0:T(8,128)S(1)} fusion(f32[1024,1024]{0,1:T(8,128)S(1)} %fusion), kind=kOutput, calls=%fused_computation.14 | convolution fusion | flops 1612578816 | bytes 4718592 | tf_op jit(solution)/shard_map/dot_general | solution.py:27
  99.2 8.6 %gather_fusion = f32[1024,1024]{1,0:T(8,128)} fusion(f32[1024,1024]{0,1:T(8,128)} %get-tuple-element.8, s32[1024]{0:T(1024)S(1)} %get-tuple-element.30), kind=kCustom, calls=%fused_computation.clone | custom fusion | bytes 8392704 | tf_op jit(solution)/shard_map/jit(_take)/gather | solution.py:46
  107.8 8.6 %gather_fusion.1 = f32[1024,1024]{1,0:T(8,128)} fusion(f32[1024,1024]{0,1:T(8,128)} %get-tuple-element.8, s32[1024]{0:T(1024)S(1)} %get-tuple-element.31), kind=kCustom, calls=%fused_computation.1.clone | custom fusion | bytes 8392704 | tf_op jit(solution)/shard_map/jit(_take)/gather | solution.py:47
  116.4 4.0 %fusion.1 = f32[1024,1024]{0,1:T(8,128)S(1)} fusion(f32[1024,1024]{1,0:T(8,128)} %gather_fusion.1, f32[1024,1024]{1,0:T(8,128)} %gather_fusion, f32[1024]{0:T(1024)S(1)} %bitcast.248, f32[1024]{0:T(1024)S(1)} %bitcast.247, pred[1024]{0:T(1024)(128)(4,1)S(1)} %get-tuple-element.29, pred[1024]{0:T(1024)(128)(4,1)S(1)} %get-tuple-element.28), kind=kLoop, calls=%fused_computation.10 | loop fusion | flops 5242880 | bytes 12593152 | tf_op jit(solution)/shard_map/add | solution.py:48
  120.4 8.5 %fusion.34 = f32[1024,128]{1,0:T(8,128)S(1)} fusion(f32[1024,1024]{0,1:T(8,128)S(1)} %fusion.1), kind=kOutput, calls=%fused_computation.70 | convolution fusion | flops 1612447744 | bytes 4718592 | tf_op jit(solution)/shard_map/dot_general | solution.py:27
  128.9 8.9 %convolution_negate_fusion.1 = f32[1024,128]{1,0:T(8,128)S(1)} fusion(f32[1024,1024]{0,1:T(8,128)S(1)} %fusion.1), kind=kOutput, calls=%fused_computation.15 | convolution fusion | flops 1612578816 | bytes 4718592 | tf_op jit(solution)/shard_map/dot_general | solution.py:27
  137.9 3.0 fusion.42
  140.9 3.0 fusion.40
  143.9 3.0 fusion.3
  146.9 3.0 fusion.2
  149.9 3.0 fusion.46
  152.9 3.2 %fusion.44 = f32[128,128]{1,0:T(8,128)S(1)} fusion(f32[1024,128]{1,0:T(8,128)S(1)} %convolution_negate_fusion.1, s32[128]{0:T(128)S(1)} %iota_add_fusion), kind=kOutput, calls=%fused_computation.75 | convolution fusion | flops 203161600 | bytes 590336 | tf_op jit(solution)/shard_map/dot_general | solution.py:27
  156.1 3.0 fusion.5
  159.1 3.0 fusion.4
  168.7 91.1 %all-reduce.4.cloned.1.call-done = (f32[2,2,128,128]{3,2,1,0:T(8,128)}, f32[2,128,128]{2,1,0:T(8,128)}, f32[2,128,128]{2,1,0:T(8,128)}) async-done(((f32[2,2,128,128]{3,2,1,0:T(8,128)}, f32[2,128,128]{2,1,0:T(8,128)}, f32[2,128,128]{2,1,0:T(8,128)}), (f32[2,2,128,128]{3,2,1,0:T(8,128)}, f32[2,128,128]{2,1,0:T(8,128)}, f32[2,128,128]{2,1,0:T(8,128)})) %all-reduce.4.cloned.1.call-update) | async-done | bytes 524304 | tf_op jit(solution)/shard_map/psum | solution.py:113
  259.8 1.7 multiply_subtract_fusion.1
  271.8 32.3 %pmax.7 = f32[2]{0:T(128)} all-reduce(f32[2]{0:T(128)S(1)} %pad_maximum_fusion.2), channel_id=1, replica_groups=mesh['grp'=2,'slab'=16] {'slab'}, use_global_device_ids=true, to_apply=%region_9.11 | all-reduce | flops 2 | bytes 16 | tf_op jit(solution)/shard_map/pmax | solution.py:125
  (41 shorter events, 15.9 us)
Async XLA Ops:
  7.2 252.6 %all-reduce.4.cloned.1.call-start = ((), (), s32[]{:S(2)}) async-start(), calls=%async_computation | async-start | bytes 1048576 | tf_op jit(solution)/shard_map/psum | solution.py:113
  56.4 8.6 %copy-start.1 = (f32[2,1024]{1,0:T(2,128)S(1)}, f32[2,1024]{1,0:T(2,128)}, u32[]{:S(2)}) copy-start(f32[2,1024]{1,0:T(2,128)} %param.14) | copy-start | bytes 24580
  149.9 12.2 %copy-start.3 = (s32[16]{0:T(128)S(1)}, s32[16]{0:T(128)}, u32[]{:S(2)}) copy-start(s32[16]{0:T(128)} %param.16) | copy-start | bytes 196
  152.9 11.8 %copy-start = (f32[1,2,128,128]{3,2,1,0:T(8,128)S(1)}, f32[1,2,128,128]{3,2,1,0:T(8,128)}, u32[]{:S(2)}) copy-start(f32[1,2,128,128]{3,2,1,0:T(8,128)} %param.17) | copy-start | bytes 393220
  152.9 12.6 %copy-start.2 = (s32[2,2]{1,0:T(2,128)S(1)}, s32[2,2]{1,0:T(2,128)}, u32[]{:S(2)}) copy-start(s32[2,2]{1,0:T(2,128)} %param.15) | copy-start | bytes 52
Sparse Core Ops, SparseCore 0:
  165.6 94.1 all-reduce.3
where the time goes:
time: 318 us; the launch traced here: 312 us
  waiting for transfers between devices  91.1 us (29%)
  matrix products  75.9 us (24%)
  local copies, waits for them, and re-layouts  50.6 us (16%)
  between operations  32.7 us (10%)
  blocking collectives  32.3 us (10%)
  other arithmetic  29 us (9%)
    psum x1, waiting for transfers between devices, per_device(): spectra = lax.psum(stacked, 'slab')  91.1 us
    dot_general x24, matrix products, matmul(): jnp.dot(first, second, precision=lax.Precision.HIGHEST, preferred_element...  75.9 us
    pmax x1, blocking collectives, per_device(): peaks = lax.pmax(jnp.stack(maxima), 'slab')  32.3 us
    gather x2, local copies, waits for them, and re-layouts, reproject(): right_values = jnp.take(summed, left_cols + 1, axis=1)  17.2 us
    gather x2, local copies, waits for them, and re-layouts, reproject(): left_values = jnp.take(summed, left_cols, axis=1)  17.2 us
    add x1, other arithmetic, reproject(): summed + (1.0 - weights[plane_no]) * near_cells  12.6 us
    add x2, other arithmetic, reproject(): return (1.0 - right_share) * left_values + right_share * right_values  8.41 us
  transfers between devices with their start and end apart: 1, of which 1 were waited for; matrix products, arithmetic and copies ran while one was open for 1% of the time, Pallas kernels for 0%

commit v1 on v0

--- a/solution.py
+++ b/solution.py
@@ -110,7 +110,10 @@
         partials.append(band_part(rows_term(0, Y)))
     stacked = jnp.stack(partials)
     mine = reference_band[0]
-    spectra = lax.psum(stacked, "slab")
+    size, spectra = (lax.axis_size("slab"), stacked)
+    for stride in [1 << k for k in range(size.bit_length() - 1)]:
+        route = [(i, i ^ stride) for i in range(size)]
+        spectra = spectra + lax.ppermute(spectra, "slab", route)
     references = jnp.stack([from_root(mine, "slab", tilt_owner[which]) for which in range(TILTS)])
     total_rows = WIN_ROWS_DEV * devices
     outputs = []

time: 318 us -> 329 us (1.035)
  starting transfers between devices: 0.04 us -> 8.05 us
  waiting for transfers between devices: 91.1 us -> 95.9 us
    ppermute x0 -> x4, waiting for transfers between devices: none -> 19.6 us  [per_device(): spectra = spectra + lax.ppermute(spectra, 'slab', route)]
    psum x1, waiting for transfers between devices: 91.1 us -> 76.3 us  [from_root(): return lax.psum(kept, axis)]
    ppermute x0 -> x4, starting transfers between devices: none -> 8.01 us  [per_device(): spectra = spectra + lax.ppermute(spectra, 'slab', route)]
  transfers between devices with their start and end apart: 1 -> 5, of which waited for: 1 -> 5; matrix products, arithmetic and copies ran while one was open for 1% -> 1% of each run, Pallas kernels for 0% -> 0%
where the time goes in v1:
time: 329 us; the launch traced here: 324 us
  waiting for transfers between devices  95.9 us (29%)
  matrix products  75.9 us (23%)
  local copies, waits for them, and re-layouts  50.5 us (15%)
  between operations  32.5 us (10%)
  blocking collectives  32.4 us (10%)
  other arithmetic  28.3 us (9%)
  starting transfers between devices  8.05 us (2%)
    psum x1, waiting for transfers between devices, from_root(): return lax.psum(kept, axis)  76.3 us
    dot_general x24, matrix products, matmul(): jnp.dot(first, second, precision=lax.Precision.HIGHEST, preferred_element...  75.9 us
    pmax x1, blocking collectives, per_device(): peaks = lax.pmax(jnp.stack(maxima), 'slab')  32.4 us
    ppermute x4, waiting for transfers between devices, per_device(): spectra = spectra + lax.ppermute(spectra, 'slab', route)  19.6 us
    gather x2, local copies, waits for them, and re-layouts, reproject(): right_values = jnp.take(summed, left_cols + 1, axis=1)  17.2 us
    gather x2, local copies, waits for them, and re-layouts, reproject(): left_values = jnp.take(summed, left_cols, axis=1)  17.2 us
    add x1, other arithmetic, reproject(): summed + (1.0 - weights[plane_no]) * near_cells  12.7 us
    add x2, other arithmetic, reproject(): return (1.0 - right_share) * left_values + right_share * right_values  8.41 us
  transfers between devices with their start and end apart: 5, of which 5 were waited for; matrix products, arithmetic and copies ran while one was open for 1% of the time, Pallas kernels for 0%

profile of v1, /device:TPU:0, one launch (start us, length us, event | category | flops | bytes accessed | tf_op | source)
XLA Modules:
  0.0 323.6 jit_solution(12975801401625733191)
XLA Ops:
  23.8 6.2 %copy.10 = bf16[2,1024,1024]{1,2,0:T(8,128)(2,1)} copy(bf16[2,1024,1024]{2,1,0:T(8,128)(2,1)} %param.10) | data formatting | bytes 8388608 | tf_op args[0]
  30.0 5.0 %pad_slice_fusion.1 = (bf16[1,1024,1154]{1,2,0:T(8,128)(2,1)S(1)}, bf16[1,1024,1154]{1,2,0:T(8,128)(2,1)}) fusion(bf16[2,1024,1024]{1,2,0:T(8,128)(2,1)} %copy.10), kind=kLoop, calls=%fused_computation.5 | loop fusion | bytes 8921088 | tf_op jit(solution)/shard_map/slice | solution.py:38
  35.0 12.7 %add_bitcast_fusion.1 = (f32[1024,1024]{0,1:T(8,128)}, f32[1024,1024]{0,1:T(8,128)}) fusion(bf16[1,1024,1154]{1,2,0:T(8,128)(2,1)} %get-tuple-element.10, s32[]{:T(128)S(6)} %select_n.127, f32[]{:T(128)} %bitcast.11, s32[]{:T(128)S(6)} %select_n.126, f32[]{:T(128)S(6)} %sub.140, bf16[1,1024,1154]{1,2,0:T(8,128)(2,1)S(1)} %get-tuple-element.9, ...), kind=kLoop, calls=%fused_computation.13 | loop fusion | flops 23068672 | bytes 25165888 | tf_op jit(solution)/shard_map/add | solution.py:45
  47.7 8.6 %gather_fusion.2 = f32[1024,1024]{1,0:T(8,128)} fusion(f32[1024,1024]{0,1:T(8,128)} %get-tuple-element.8, s32[1024]{0:T(1024)S(1)} %get-tuple-element.33), kind=kCustom, calls=%fused_computation.2.clone | custom fusion | bytes 8392704 | tf_op jit(solution)/shard_map/jit(_take)/gather | solution.py:46
  56.3 8.6 %gather_fusion.3 = f32[1024,1024]{1,0:T(8,128)} fusion(f32[1024,1024]{0,1:T(8,128)} %get-tuple-element.8, s32[1024]{0:T(1024)S(1)} %get-tuple-element.34), kind=kCustom, calls=%fused_computation.3.clone | custom fusion | bytes 8392704 | tf_op jit(solution)/shard_map/jit(_take)/gather | solution.py:47
  64.9 4.4 %fusion = f32[1024,1024]{0,1:T(8,128)S(1)} fusion(f32[1024,1024]{1,0:T(8,128)} %gather_fusion.3, f32[1024,1024]{1,0:T(8,128)} %gather_fusion.2, f32[1024]{0:T(1024)S(1)} %bitcast.250, f32[1024]{0:T(1024)S(1)} %bitcast.249, pred[1024]{0:T(1024)(128)(4,1)S(1)} %get-tuple-element.32, pred[1024]{0:T(1024)(128)(4,1)S(1)} %get-tuple-element.31), kind=kLoop, calls=%fused_computation.7 | loop fusion | flops 5242880 | bytes 12593152 | tf_op jit(solution)/shard_map/add | solution.py:48
  69.3 8.5 %fusion.32 = f32[1024,128]{1,0:T(8,128)S(1)} fusion(f32[1024,1024]{0,1:T(8,128)S(1)} %fusion), kind=kOutput, calls=%fused_computation.69 | convolution fusion | flops 1612447744 | bytes 4718592 | tf_op jit(solution)/shard_map/dot_general | solution.py:27
  77.8 21.3 %convolution_negate_fusion = f32[1024,128]{1,0:T(8,128)S(1)} fusion(f32[1024,1024]{0,1:T(8,128)S(1)} %fusion), kind=kOutput, calls=%fused_computation.14 | convolution fusion | flops 1612578816 | bytes 4718592 | tf_op jit(solution)/shard_map/dot_general | solution.py:27
  99.2 8.6 %gather_fusion = f32[1024,1024]{1,0:T(8,128)} fusion(f32[1024,1024]{0,1:T(8,128)} %get-tuple-element.7, s32[1024]{0:T(1024)S(1)} %get-tuple-element.29), kind=kCustom, calls=%fused_computation.clone | custom fusion | bytes 8392704 | tf_op jit(solution)/shard_map/jit(_take)/gather | solution.py:46
  107.8 8.6 %gather_fusion.1 = f32[1024,1024]{1,0:T(8,128)} fusion(f32[1024,1024]{0,1:T(8,128)} %get-tuple-element.7, s32[1024]{0:T(1024)S(1)} %get-tuple-element.30), kind=kCustom, calls=%fused_computation.1.clone | custom fusion | bytes 8392704 | tf_op jit(solution)/shard_map/jit(_take)/gather | solution.py:47
  116.4 4.0 %fusion.1 = f32[1024,1024]{0,1:T(8,128)S(1)} fusion(f32[1024,1024]{1,0:T(8,128)} %gather_fusion.1, f32[1024,1024]{1,0:T(8,128)} %gather_fusion, f32[1024]{0:T(1024)S(1)} %bitcast.248, f32[1024]{0:T(1024)S(1)} %bitcast.247, pred[1024]{0:T(1024)(128)(4,1)S(1)} %get-tuple-element.28, pred[1024]{0:T(1024)(128)(4,1)S(1)} %get-tuple-element.27), kind=kLoop, calls=%fused_computation.10 | loop fusion | flops 5242880 | bytes 12593152 | tf_op jit(solution)/shard_map/add | solution.py:48
  120.4 8.5 %fusion.34 = f32[1024,128]{1,0:T(8,128)S(1)} fusion(f32[1024,1024]{0,1:T(8,128)S(1)} %fusion.1), kind=kOutput, calls=%fused_computation.70 | convolution fusion | flops 1612447744 | bytes 4718592 | tf_op jit(solution)/shard_map/dot_general | solution.py:27
  128.9 8.9 %convolution_negate_fusion.1 = f32[1024,128]{1,0:T(8,128)S(1)} fusion(f32[1024,1024]{0,1:T(8,128)S(1)} %fusion.1), kind=kOutput, calls=%fused_computation.15 | convolution fusion | flops 1612578816 | bytes 4718592 | tf_op jit(solution)/shard_map/dot_general | solution.py:27
  143.8 3.0 fusion.3
  146.8 3.0 fusion.2
  149.8 3.0 fusion.46
  152.8 3.2 fusion.44
  156.0 3.0 fusion.5
  159.1 3.0 fusion.4
  166.8 6.6 %collective-permute-done.1 = f32[2,2,128,128]{3,2,1,0:T(8,128)S(1)} collective-permute-done((f32[2,2,128,128]{3,2,1,0:T(8,128)S(1)}, f32[2,2,128,128]{3,2,1,0:T(8,128)S(1)}, u32[]{:S(2)}, u32[]{:S(2)}) %collective-permute-start.1) | collective-permute-done | bytes 262176 | tf_op jit(solution)/shard_map/ppermute | solution.py:116
  177.9 3.4 %collective-permute-done.2 = f32[2,2,128,128]{3,2,1,0:T(8,128)S(1)} collective-permute-done((f32[2,2,128,128]{3,2,1,0:T(8,128)S(1)}, f32[2,2,128,128]{3,2,1,0:T(8,128)S(1)}, u32[]{:S(2)}, u32[]{:S(2)}) %collective-permute-start.2) | collective-permute-done | bytes 262176 | tf_op jit(solution)/shard_map/ppermute | solution.py:116
  187.1 8.4 %collective-permute-done.3 = f32[2,2,128,128]{3,2,1,0:T(8,128)S(1)} collective-permute-done((f32[2,2,128,128]{3,2,1,0:T(8,128)S(1)}, f32[2,2,128,128]{3,2,1,0:T(8,128)S(1)}, u32[]{:S(2)}, u32[]{:S(2)}) %collective-permute-start.3) | collective-permute-done | bytes 262176 | tf_op jit(solution)/shard_map/ppermute | solution.py:116
  195.6 76.3 %all-reduce.4.cloned.1.call-done = (f32[2,128,128]{2,1,0:T(8,128)}, f32[2,128,128]{2,1,0:T(8,128)}) async-done(((f32[2,128,128]{2,1,0:T(8,128)}, f32[2,128,128]{2,1,0:T(8,128)}), (f32[2,128,128]{2,1,0:T(8,128)}, f32[2,128,128]{2,1,0:T(8,128)})) %all-reduce.4.cloned.1.call-update) | async-done | bytes 262160 | tf_op jit(solution)/shard_map/psum | solution.py:17
  283.6 32.4 %pmax.7 = f32[2]{0:T(128)} all-reduce(f32[2]{0:T(128)S(1)} %pad_maximum_fusion.2), channel_id=1, replica_groups=mesh['grp'=2,'slab'=16] {'slab'}, use_global_device_ids=true, to_apply=%region_8.10 | all-reduce | flops 2 | bytes 16 | tf_op jit(solution)/shard_map/pmax | solution.py:128
  (53 shorter events, 31.9 us)
Async XLA Ops:
  7.2 264.7 %all-reduce.4.cloned.1.call-start = ((), (), s32[]{:S(2)}) async-start(), calls=%async_computation | async-start | bytes 524288 | tf_op jit(solution)/shard_map/psum | solution.py:17
  56.3 8.6 %copy-start.1 = (f32[2,1024]{1,0:T(2,128)S(1)}, f32[2,1024]{1,0:T(2,128)}, u32[]{:S(2)}) copy-start(f32[2,1024]{1,0:T(2,128)} %param.14) | copy-start | bytes 24580
  156.0 19.4 %copy-start.3 = (s32[16]{0:T(128)S(1)}, s32[16]{0:T(128)}, u32[]{:S(2)}) copy-start(s32[16]{0:T(128)} %param.16) | copy-start | bytes 196
  156.0 21.1 %copy-start = (f32[1,2,128,128]{3,2,1,0:T(8,128)S(1)}, f32[1,2,128,128]{3,2,1,0:T(8,128)}, u32[]{:S(2)}) copy-start(f32[1,2,128,128]{3,2,1,0:T(8,128)} %param.17) | copy-start | bytes 393220
  156.0 27.9 %copy-start.2 = (s32[2,2]{1,0:T(2,128)S(1)}, s32[2,2]{1,0:T(2,128)}, u32[]{:S(2)}) copy-start(s32[2,2]{1,0:T(2,128)} %param.15) | copy-start | bytes 52
  162.1 1.7 collective-permute-start
  163.9 9.5 %collective-permute-start.1 = (f32[2,2,128,128]{3,2,1,0:T(8,128)S(1)}, f32[2,2,128,128]{3,2,1,0:T(8,128)S(1)}, u32[]{:S(2)}, u32[]{:S(2)}) collective-permute-start(f32[2,2,128,128]{3,2,1,0:T(8,128)S(1)} %fusion.198), channel_id=1, source_target_pairs={{0,2},{1,3},{2,0},{3,1},{4,6},{5,7},{6,4},{7,5},{8,10},{9,11},{10,... | collective-permute-start | bytes 786440 | tf_op jit(solution)/shard_map/ppermute | solution.py:116
  173.5 7.8 %collective-permute-start.2 = (f32[2,2,128,128]{3,2,1,0:T(8,128)S(1)}, f32[2,2,128,128]{3,2,1,0:T(8,128)S(1)}, u32[]{:S(2)}, u32[]{:S(2)}) collective-permute-start(f32[2,2,128,128]{3,2,1,0:T(8,128)S(1)} %fusion.238), channel_id=1, source_target_pairs={{0,4},{1,5},{2,6},{3,7},{4,0},{5,1},{6,2},{7,3},{8,12},{9,13},{10,... | collective-permute-start | bytes 786440 | tf_op jit(solution)/shard_map/ppermute | solution.py:116
  181.3 14.2 %collective-permute-start.3 = (f32[2,2,128,128]{3,2,1,0:T(8,128)S(1)}, f32[2,2,128,128]{3,2,1,0:T(8,128)S(1)}, u32[]{:S(2)}, u32[]{:S(2)}) collective-permute-start(f32[2,2,128,128]{3,2,1,0:T(8,128)S(1)} %add.327), channel_id=1, source_target_pairs={{0,8},{1,9},{2,10},{3,11},{4,12},{5,13},{6,14},{7,15},{8,0},{9,1},... | collective-permute-start | bytes 786440 | tf_op jit(solution)/shard_map/ppermute | solution.py:116
Sparse Core Ops, SparseCore 0:
  178.0 93.8 all-reduce.3
